TPU v7x, 32 devices: a whole 2x2x4 slice. The times are simulated.
32 devices in a mesh: row: 2 (over y), phi: 16 (over z, x, core).
Axes of the slice: x: 2, y: 2, z: 4, core: 2. Of those that a mesh axis runs over, the one named last changes fastest.
Arguments:
- density: float32 [32, 2048, 512], P('row', 'phi'), may hold values from 0.3 to 3
- velocity: float32 [3, 32, 2048, 512], P(None, 'row', 'phi'), may hold values from -3 to 3
- magnetic: float32 [3, 32, 2048, 512], P(None, 'row', 'phi'), may hold values from -6 to 6
Outputs:
- density_next: float32 [32, 2048, 512], P('row', 'phi')
- magnetic_next: float32 [3, 32, 2048, 512], P(None, 'row', 'phi')
All inputs are finite; a program needn't handle non-finite values.
Results may differ from a plain program's by a relative error of at most 0.0003.
Values sent between devices are 32-bit elements; how exact they have to be, the bound alone decides.
A program may use at most 256 MiB of HBM per device.

v0:
```python
from functools import partial
import jax
import jax.numpy as jnp
from jax import lax
from jax.sharding import PartitionSpec as P

NP = 2048
NPOL = 128
COURANT_RAD = 0.3
COURANT_POL = 0.25
COURANT_AZI = 0.35
SOUND_SPEED = 1.0


def extended(value, sides, width, wrap):
    for axis, dim in sides:
        devices, length = (lax.axis_size(axis), value.shape[dim])
        up = [(i, (i + 1) % devices) for i in range(devices if wrap else devices - 1)]
        down = [(j, i) for i, j in up]
        last = lax.slice_in_dim(value, length - width, length, axis=dim)
        leading = lax.slice_in_dim(value, 0, width, axis=dim)
        before = lax.ppermute(last, axis, up)
        after = lax.ppermute(leading, axis, down)
        value = jnp.concatenate([before, value, after], axis=dim)
    return value


def shift_theta(values, offset):
    if offset == 0:
        return values
    if offset > 0:
        border = jnp.repeat(values[..., -1:], offset, axis=-1)
        return jnp.concatenate([values[..., offset:], border], axis=-1)
    border = jnp.repeat(values[..., :1], -offset, axis=-1)
    return jnp.concatenate([border, values[..., :offset]], axis=-1)


def interface_value(outer_left, inner_left, inner_right, outer_right):
    guess = 7.0 / 12.0 * (inner_left + inner_right) - 1.0 / 12.0 * (outer_left + outer_right)
    return jnp.clip(
        guess, jnp.minimum(inner_left, inner_right), jnp.maximum(inner_left, inner_right)
    )


def edge_values(nearby):
    centre = nearby(0)
    left_face = interface_value(nearby(-2), nearby(-1), centre, nearby(1))
    right_face = interface_value(nearby(-1), centre, nearby(1), nearby(2))
    to_left = left_face - centre
    to_right = right_face - centre
    left_limited = jnp.clip(to_left, -2.0 * jnp.abs(to_right), 2.0 * jnp.abs(to_right))
    right_limited = jnp.clip(to_right, -2.0 * jnp.abs(to_left), 2.0 * jnp.abs(to_left))
    return (centre + left_limited, centre + right_limited)


def hll_flux(dens_left, dens_right, speed_left, speed_right):
    slowest = jnp.minimum(jnp.minimum(speed_left, speed_right) - SOUND_SPEED, 0.0)
    fastest = jnp.maximum(jnp.maximum(speed_left, speed_right) + SOUND_SPEED, 0.0)
    upwind = fastest * dens_left * speed_left - slowest * dens_right * speed_right
    return (upwind + slowest * fastest * (dens_right - dens_left)) / (fastest - slowest)


def axis_divergence(dens, speed, axis, count, ghost):

    def picker(field):

        def nearby(offset):
            return lax.slice_in_dim(
                field, ghost - 1 + offset, ghost + 1 + offset + count, axis=axis
            )

        return nearby

    def window(values, start, stop):
        return lax.slice_in_dim(values, start, stop, axis=axis)

    dens_left, dens_right = edge_values(picker(dens))
    speed_left, speed_right = edge_values(picker(speed))
    flux = hll_flux(
        window(dens_right, 0, count + 1),
        window(dens_left, 1, count + 2),
        window(speed_right, 0, count + 1),
        window(speed_left, 1, count + 2),
    )
    return window(flux, 1, count + 1) - window(flux, 0, count)


def theta_divergence(dens, speed):
    dens_left, dens_right = edge_values(partial(shift_theta, dens))
    speed_left, speed_right = edge_values(partial(shift_theta, speed))
    flux = hll_flux(
        shift_theta(dens_right, -1), dens_left, shift_theta(speed_right, -1), speed_left
    )
    position = lax.broadcasted_iota(jnp.int32, flux.shape, flux.ndim - 1)
    flux = jnp.where(position == 0, jnp.zeros_like(flux), flux)
    upper_flux = jnp.concatenate([flux[..., 1:], jnp.zeros_like(flux[..., :1])], axis=-1)
    return upper_flux - flux


def advance(primitive, magnetic, ghost, face_ghost, radial, azimuth):
    dens = primitive[0]
    radial_speed = primitive[1]
    polar_speed = primitive[2]
    azimuth_speed = primitive[3]

    def inner(values, width):
        return values[width : width + radial, width : width + azimuth]

    def box(values, width):
        return values[width - 1 : width + radial + 1, width - 1 : width + azimuth + 1]

    rad_term = axis_divergence(
        dens[:, ghost : ghost + azimuth], radial_speed[:, ghost : ghost + azimuth], 0, radial, ghost
    )
    azi_term = axis_divergence(
        dens[ghost : ghost + radial], azimuth_speed[ghost : ghost + radial], 1, azimuth, ghost
    )
    dens_inner = inner(dens, ghost)
    pol_term = theta_divergence(dens_inner, inner(polar_speed, ghost))
    density_next = (
        dens_inner - COURANT_RAD * rad_term - COURANT_POL * pol_term - COURANT_AZI * azi_term
    )
    radial_span = magnetic[0][
        face_ghost - 1 : face_ghost + radial + 2, face_ghost - 1 : face_ghost + azimuth + 1
    ]
    radial_cell = 0.5 * (radial_span[:-1] + radial_span[1:])
    azimuth_span = magnetic[2][
        face_ghost - 1 : face_ghost + radial + 1, face_ghost - 1 : face_ghost + azimuth + 2
    ]
    azimuth_cell = 0.5 * (azimuth_span[:, :-1] + azimuth_span[:, 1:])
    polar_box = box(magnetic[1], face_ghost)
    polar_cell = 0.5 * (polar_box + shift_theta(polar_box, 1))
    speed_r = box(radial_speed, ghost)
    speed_t = box(polar_speed, ghost)
    speed_p = box(azimuth_speed, ghost)
    radial_emf = -(speed_t * azimuth_cell - speed_p * polar_cell)
    polar_emf = -(speed_p * radial_cell - speed_r * azimuth_cell)
    azimuth_emf = -(speed_r * polar_cell - speed_t * radial_cell)
    radial_edge = 0.5 * (radial_emf[1 : radial + 1, :-1] + radial_emf[1 : radial + 1, 1:])
    radial_below = 0.5 * (shift_theta(radial_edge, -1) + radial_edge)
    radial_above = 0.5 * (radial_edge + shift_theta(radial_edge, 1))
    azimuth_edge = 0.5 * (azimuth_emf[:-1, 1 : azimuth + 1] + azimuth_emf[1:, 1 : azimuth + 1])
    azimuth_below = 0.5 * (shift_theta(azimuth_edge, -1) + azimuth_edge)
    azimuth_above = 0.5 * (azimuth_edge + shift_theta(azimuth_edge, 1))
    polar_edge = 0.25 * (
        polar_emf[:-1, :-1] + polar_emf[1:, :-1] + polar_emf[:-1, 1:] + polar_emf[1:, 1:]
    )
    radial_next = (
        inner(magnetic[0], face_ghost)
        - COURANT_POL * (azimuth_above[:radial] - azimuth_below[:radial])
        + COURANT_AZI * (polar_edge[:radial, 1:] - polar_edge[:radial, :-1])
    )
    polar_next = (
        inner(magnetic[1], face_ghost)
        - COURANT_AZI * (radial_below[:, 1:] - radial_below[:, :-1])
        + COURANT_RAD * (azimuth_below[1:] - azimuth_below[:-1])
    )
    azimuth_next = (
        inner(magnetic[2], face_ghost)
        - COURANT_RAD * (polar_edge[1:, :azimuth] - polar_edge[:-1, :azimuth])
        + COURANT_POL * (radial_above[:, :azimuth] - radial_below[:, :azimuth])
    )
    return (density_next, jnp.stack([radial_next, polar_next, azimuth_next]))


def radial_fix(padded, width):
    first_row = lax.axis_index("row") == 0
    last_row = lax.axis_index("row") == lax.axis_size("row") - 1
    inner_low = jnp.broadcast_to(padded[:, width : width + 1], padded[:, :width].shape)
    inner_high = jnp.broadcast_to(padded[:, -width - 1 : -width], padded[:, -width:].shape)
    low_side = jnp.where(first_row, inner_low, padded[:, :width])
    high_side = jnp.where(last_row, inner_high, padded[:, -width:])
    return jnp.concatenate([low_side, padded[:, width:-width], high_side], axis=1)


def ghost_state(values):
    padded = radial_fix(extended(values, (("row", 1),), 3, False), 3)
    result = extended(padded, (("phi", 2),), 3, True)
    return result


def per_device(density, velocity, magnetic):
    radial, azimuth, theta_count = density.shape
    half_polar = NPOL // 2
    primitive = jnp.concatenate([density[None], velocity], axis=0)
    polar_rows = jnp.concatenate(
        [primitive[..., :half_polar], primitive[..., theta_count - half_polar :]], axis=-1
    )
    polar_rows = jnp.swapaxes(polar_rows, 2, 3)
    column = lax.broadcasted_iota(jnp.int32, (NP, NP), 1)
    sample = lax.broadcasted_iota(jnp.int32, (NP, NP), 0)
    mode_index = jnp.where(column <= NP // 2, column, column - NP // 2)
    phase_angle = (sample * mode_index % NP).astype(jnp.float32) * (2.0 * jnp.pi / NP)
    fourier_basis = jnp.where(column <= NP // 2, jnp.cos(phase_angle), jnp.sin(phase_angle))
    mode_row = mode_index[0]
    column_row = column[0]
    weights = jnp.where((mode_row == 0) | (column_row == NP // 2), 1.0 / NP, 2.0 / NP).astype(
        jnp.float32
    )
    mode_sine = jnp.sin(jnp.pi * mode_row.astype(jnp.float32) / NP)
    edge_sine = jnp.sin(jnp.pi * (half_polar + 0.5) / theta_count)
    lines = lax.all_to_all(polar_rows, "phi", split_axis=2, concat_axis=3, tiled=True)
    local_rows = lines.shape[2]
    global_row = lax.axis_index("phi") * local_rows + jnp.arange(local_rows, dtype=jnp.int32)
    theta_row = jnp.where(global_row < half_polar, global_row, theta_count - NPOL + global_row)
    row_sine = jnp.sin(jnp.pi * (theta_row.astype(jnp.float32) + 0.5) / theta_count)
    row_square = (row_sine * row_sine)[:, None]
    mode_square = (edge_sine * mode_sine)[None, :]
    damping = row_square / jnp.maximum(row_square, mode_square * mode_square)
    spectrum = jnp.dot(
        lines.reshape(-1, NP),
        fourier_basis,
        precision=lax.Precision.HIGHEST,
        preferred_element_type=jnp.float32,
    ).reshape(lines.shape)
    spectrum = spectrum * (damping * weights[None, :])
    smoothed = lax.dot_general(
        spectrum.reshape(-1, NP),
        fourier_basis,
        (((1,), (1,)), ((), ())),
        precision=lax.Precision.HIGHEST,
        preferred_element_type=jnp.float32,
    ).reshape(lines.shape)
    returned = lax.all_to_all(smoothed, "phi", split_axis=3, concat_axis=2, tiled=True)
    returned = jnp.swapaxes(returned, 2, 3)
    primitive = jnp.concatenate(
        [
            returned[..., :half_polar],
            primitive[..., half_polar : theta_count - half_polar],
            returned[..., half_polar:],
        ],
        axis=-1,
    )
    state = ghost_state(jnp.concatenate([primitive, magnetic], axis=0))
    primitive_padded = state[:4]
    magnetic_padded = state[4:]
    face_ghost = 3
    return advance(primitive_padded, magnetic_padded, 3, face_ghost, radial, azimuth)


def solution(mesh):
    placed = (P("row", "phi", None), P(None, "row", "phi", None), P(None, "row", "phi", None))
    return jax.shard_map(
        per_device,
        mesh=mesh,
        in_specs=placed,
        out_specs=(P("row", "phi", None), P(None, "row", "phi", None)),
        check_vma=False,
    )
```

profile of v0, /device:TPU:13, one launch (start us, length us, event | category | flops | bytes accessed | tf_op | source)
XLA Modules:
  0.0 1016.8 jit_solution(8713738832390552506)
XLA Ops:
  20.5 67.5 %fusion.152 = f32[2048,2048,1,1]{1,0,3,2:T(8,128)} fusion(s32[2048]{0:T(1024)S(1)} %iota_add_fusion, pred[2048]{0:T(1024)(128)(4,1)S(1)} %iota_compare_fusion.2), kind=kLoop, calls=%fused_computation.10.clone.1 | loop fusion | flops 67108864 | bytes 16787456 | tf_op jit(solution)/shard_map/dot_general | solution.py:210
  88.0 20.2 %all-to-all-done = f32[4,16,128,128]{3,1,0,2:T(8,128)} async-done(((f32[4,16,128,128]{3,1,0,2:T(8,128)}), f32[4,16,128,128]{3,1,0,2:T(8,128)}, u32[]{:S(2)}, u32[]{:S(2)}) %all-to-all-start) | async-done | bytes 4194336 | tf_op jit(solution)/shard_map/all_to_all | solution.py:202
  108.2 34.1 %fusion.5 = f32[4,16,8,2048]{3,2,1,0:T(8,128)S(1)} fusion(f32[4,16,128,128]{3,1,0,2:T(8,128)} %all-to-all-done, f32[2048,2048,1,1]{1,0,3,2:T(8,128)} %fusion.152), kind=kOutput, calls=%fused_computation.9 | convolution fusion | flops 25769803776 | bytes 25165824 | tf_op jit(solution)/shard_map/dot_general | solution.py:210
  142.6 94.4 %fusion.3 = f32[4,16,8,2048]{3,2,1,0:T(8,128)} fusion(pred[2048]{0:T(1024)(128)(4,1)S(1)} %iota_compare_fusion.2, s32[2048]{0:T(1024)S(1)} %iota_add_fusion, f32[4,16,8,2048]{3,2,1,0:T(8,128)S(1)} %fusion.150), kind=kOutput, calls=%fused_computation.7 | convolution fusion | flops 25836912640 | bytes 8398848 | tf_op jit(solution)/shard_map/dot_general | solution.py:217
  237.0 26.4 %copy.108 = f32[4,16,8,2048]{1,2,0,3:T(8,128)} copy(f32[4,16,8,2048]{3,2,1,0:T(8,128)} %fusion.3) | data formatting | bytes 8388608 | tf_op jit(solution)/shard_map/dot_general | solution.py:217
  263.4 22.0 %reshape.119 = f32[16,1,65536]{2,1,0:T(1,128)} reshape(f32[2048,4,8,16]{3,2,1,0:T(8,128)} %bitcast.95) | data formatting | bytes 8388608
  292.4 11.6 %pad_maximum_fusion.1 = f32[4,16,128,384]{3,2,0,1:T(8,128)} fusion(f32[1,16,128,512]{3,2,0,1:T(8,128)} %bitcast.114, f32[3,16,128,512]{3,2,1,0:T(8,128)} %param.4), kind=kLoop, calls=%fused_computation.13 | loop fusion | flops 3145728 | bytes 29360128 | tf_op jit(solution)/shard_map/concatenate | solution.py:185
  304.0 78.6 %all-to-all-done.1 = f32[16,1,65536]{2,1,0:T(1,128)} async-done(((f32[16,1,65536]{2,1,0:T(1,128)}), f32[16,1,65536]{2,1,0:T(1,128)}, u32[]{:S(2)}, u32[]{:S(2)}) %all-to-all-start.1) | async-done | bytes 4194336 | tf_op jit(solution)/shard_map/all_to_all | solution.py:224
  383.1 13.7 %reduce.8 = f32[16,65536]{1,0:T(8,128)} reduce(f32[16,1,65536]{2,1,0:T(1,128)} %all-to-all-done.1, f32[]{:T(128)} %broadcast.356), dimensions={1}, to_apply=%all_to_all.27.reduce_sub_computation | reduce | bytes 8388612 | tf_op jit(solution)/shard_map/all_to_all | solution.py:224
  396.8 25.8 %reshape.120 = f32[2048,4,8,16]{3,2,1,0:T(8,128)} reshape(f32[16,65536]{1,0:T(8,128)} %reduce.8) | data formatting | bytes 8388608
  422.6 21.1 %copy.110 = f32[4,16,16,8,128]{4,3,2,1,0:T(8,128)} copy(f32[4,16,16,8,128]{1,3,0,4,2:T(8,128)} %bitcast.96) | data formatting | bytes 8388608 | tf_op jit(solution)/shard_map/all_to_all | solution.py:224
  477.4 106.1 %collective-permute-done.1 = f32[7,3,128,512]{3,2,1,0:T(8,128)} collective-permute-done((f32[7,3,128,512]{3,2,1,0:T(8,128)}, f32[7,3,128,512]{3,2,1,0:T(8,128)}, u32[]{:S(2)}, u32[]{:S(2)}) %collective-permute-start.1) | collective-permute-done | bytes 5505056 | tf_op jit(solution)/shard_map/ppermute | solution.py:23
  611.4 21.4 %collective-permute-done.3 = f32[7,22,3,512]{3,1,2,0:T(8,128)S(1)} collective-permute-done((f32[7,22,3,512]{3,1,2,0:T(8,128)S(1)}, f32[7,22,3,512]{3,1,2,0:T(8,128)S(1)}, u32[]{:S(2)}, u32[]{:S(2)}) %collective-permute-start.3) | collective-permute-done | bytes 946208 | tf_op jit(solution)/shard_map/ppermute | solution.py:23
  636.2 57.4 %pad_maximum_fusion = f32[7,22,134,512]{3,2,0,1:T(8,128)} fusion(f32[7,22,3,512]{3,2,0,1:T(4,128)} %copy.121, f32[7,3,128,512]{3,2,0,1:T(8,128)} %copy-done.6, f32[4,16,128,64]{3,2,0,1:T(8,128)S(1)} %copy-done.2, f32[4,16,128,384]{3,2,0,1:T(8,128)S(1)} %bitcast.86, f32[4,16,128,64]{3,2,0,1:T(8,128)} %copy.111, f32[7,3,128,512]{3,2,0,1:T(8,128)} %copy_select_fusion.1, ...), kind=kLoop, calls=%fused_computation | loop fusion | flops 73959424 | bytes 84525056 | tf_op jit(solution)/shard_map/concatenate | solution.py:24
  701.9 25.3 %slice_bitcast_fusion.3 = (f32[22,134,512]{2,1,0:T(8,128)}, f32[22,134,512]{2,1,0:T(8,128)}, f32[22,134,512]{2,1,0:T(8,128)S(1)}, f32[22,134,512]{2,1,0:T(8,128)...) fusion(f32[7,22,134,512]{3,2,0,1:T(8,128)} %pad_maximum_fusion), kind=kLoop, calls=%fused_computation.18 | loop fusion | bytes 84525056 | tf_op jit(solution)/shard_map/squeeze | solution.py:149
  757.5 27.9 %fusion.15 = (f32[18,128,512]{2,1,0:T(8,128)}, f32[18,128,512]{2,1,0:T(8,128)}, f32[18,128,512]{2,1,0:T(8,128)}, f32[18,128,512]{2,1,0:T(8,128)}, f32[18,128,512]{2,1,0:T(8,128)}, /*index=5*/f32[18,128,512]{2,1,0:T(8,128)}) fusion(f32[22,134,512]{2,1,0:T(8,128)} %copy-done, f32[22,134,512]{2,1,0:T(8,128)} %get-tuple-element.21), kind=kLoop, calls=%fused_computation.46 | loop fusion | flops 47185920 | bytes 75497472 | tf_op jit(solution)/shard_map/sub | solution.py:50
  785.4 15.4 %subtract_negate_fusion.1 = f32[18,130,512]{2,1,0:T(8,128)} fusion(f32[22,134,512]{2,1,0:T(8,128)} %get-tuple-element.24, f32[22,134,512]{2,1,0:T(8,128)} %get-tuple-element.21, f32[22,134,512]{2,1,0:T(8,128)} %get-tuple-element.18, f32[22,134,512]{2,1,0:T(8,128)} %get-tuple-element.23), kind=kLoop, calls=%fused_computation.35 | loop fusion | flops 9584640 | bytes 33546240 | tf_op jit(solution)/shard_map/neg | solution.py:137
  800.8 23.7 %subtract_negate_fusion.2 = (f32[18,130,512]{2,1,0:T(8,128)}, f32[18,130,512]{2,1,0:T(8,128)}) fusion(f32[22,134,512]{2,1,0:T(8,128)} %copy-done.1, f32[22,134,512]{2,1,0:T(8,128)} %get-tuple-element.21, f32[22,134,512]{2,1,0:T(8,128)} %get-tuple-element.18, f32[18,130,1]{2,1,0:T(8,128)S(1)} %slice.613, f32[18,130,511]{2,1,0:T(8,128)} %slice.612, ...), kind=kLoop, calls=%fused_computation.36 | loop fusion | flops 17971200 | bytes 52715520 | tf_op jit(solution)/shard_map/neg | solution.py:138
  849.1 16.7 %minimum_add_fusion = (f32[16,128,512]{2,1,0:T(8,128)}, f32[16,128,512]{2,1,0:T(8,128)}) fusion(f32[16,128,2]{2,1,0:T(8,128)S(1)} %reshape.113, f32[16,128,510]{2,1,0:T(8,128)S(1)} %copy-done.9, f32[16,128,510]{2,1,0:T(8,128)S(1)} %copy-done.7, f32[16,128,2]{2,1,0:T(8,128)S(1)} %reshape.112, f32[22,134,512]{2,1,0:T(8,128)S(1)} %bitcast.84, ...), kind=kLoop, calls=%fused_computation.206 | loop fusion | flops 62914560 | bytes 50331648 | tf_op jit(solution)/shard_map/add | solution.py:53
  870.6 21.0 %divide_select_fusion = f32[16,128,512]{2,1,0:T(8,128)} fusion(f32[16,128,511]{2,1,0:T(8,128)} %bitcast.111, f32[16,128,1]{2,1,0:T(8,128)} %slice.578, f32[16,128,2]{2,1,0:T(8,128)S(1)} %reshape.113, f32[16,128,510]{2,1,0:T(8,128)} %get-tuple-element.46, f32[16,128,510]{2,1,0:T(8,128)S(1)} %copy-done.8, f32[16,128,2]{2,1,0:T(8,128)S(1)} %reshape.112, ...), kind=kLoop, calls=%fused_computation.205 | loop fusion | flops 83886080 | bytes 54526464 | tf_op jit(solution)/shard_map/jit(_where)/select_n | solution.py:95
  931.7 16.6 %subtract_divide_fusion = f32[16,129,512]{2,1,0:T(8,128)} fusion(f32[16,130,512]{2,1,0:T(8,128)S(1)} %bitcast.108, f32[16,130,512]{2,1,0:T(8,128)S(1)} %bitcast.110, f32[16,130,512]{2,1,0:T(8,128)S(1)} %bitcast.106, f32[16,130,512]{2,1,0:T(8,128)} %get-tuple-element.73, f32[16,130,512]{2,1,0:T(8,128)} %get-tuple-element.72, ...), kind=kLoop, calls=%fused_computation.131 | loop fusion | flops 43327488 | bytes 54951936 | tf_op jit(solution)/shard_map/div | solution.py:60
  948.2 20.9 %subtract_divide_fusion.1 = f32[17,128,512]{2,1,0:T(8,128)} fusion(f32[18,128,512]{2,1,0:T(8,128)} %get-tuple-element.51, f32[18,128,512]{2,1,0:T(8,128)} %get-tuple-element.52, f32[18,128,512]{2,1,0:T(8,128)} %get-tuple-element.50, f32[18,128,512]{2,1,0:T(8,128)} %get-tuple-element.76, f32[18,128,512]{2,1,0:T(8,128)} %get-tuple-element.75, ...), kind=kLoop, calls=%fused_computation.132 | loop fusion | flops 45678592 | bytes 57933824 | tf_op jit(solution)/shard_map/div | solution.py:60
  980.0 24.2 %fusion.77 = (f32[1,16,128,512]{3,2,1,0:T(8,128)}, f32[1,16,128,512]{3,2,1,0:T(8,128)}, f32[1,16,128,512]{3,2,1,0:T(8,128)}) fusion(f32[17,129,512]{2,1,0:T(8,128)} %fusion.10, f32[17,128,512]{2,1,0:T(8,128)} %copy-done.4, f32[17,128,1]{2,1,0:T(8,128)S(1)} %copy-done.12, f32[17,128,511]{2,1,0:T(8,128)} %get-tuple-element.56, ...), kind=kLoop, calls=%fused_computation.153 | loop fusion | flops 25165824 | bytes 71598080 | tf_op jit(solution)/shard_map/stack | solution.py:163
  1004.2 12.1 %pad_maximum_fusion.2 = f32[3,16,128,512]{3,2,1,0:T(8,128)} fusion(f32[1,16,128,512]{3,2,1,0:T(8,128)} %get-tuple-element.54, f32[1,16,128,512]{3,2,1,0:T(8,128)} %get-tuple-element.55, f32[1,16,128,512]{3,2,1,0:T(8,128)} %get-tuple-element.53), kind=kLoop, calls=%fused_computation.14 | loop fusion | flops 6291456 | bytes 25165824 | tf_op jit(solution)/shard_map/stack | solution.py:163
  (157 shorter events, 211.1 us)
Async XLA Ops:
  11.4 96.8 %all-to-all-start = ((f32[4,16,128,128]{3,1,0,2:T(8,128)}), f32[4,16,128,128]{3,1,0,2:T(8,128)}, u32[]{:S(2)}, u32[]{:S(2)}) async-start(f32[4,16,128,128]{3,1,0,2:T(8,128)} %copy.106), calls=%async_computation | async-start | bytes 8388608 | tf_op jit(solution)/shard_map/all_to_all | solution.py:202
  285.4 97.2 %all-to-all-start.1 = ((f32[16,1,65536]{2,1,0:T(1,128)}), f32[16,1,65536]{2,1,0:T(1,128)}, u32[]{:S(2)}, u32[]{:S(2)}) async-start(f32[16,1,65536]{2,1,0:T(1,128)} %reshape.119), calls=%async_computation.1 | async-start | bytes 8388608 | tf_op jit(solution)/shard_map/all_to_all | solution.py:224
  464.0 119.5 %collective-permute-start.1 = (f32[7,3,128,512]{3,2,1,0:T(8,128)}, f32[7,3,128,512]{3,2,1,0:T(8,128)}, u32[]{:S(2)}, u32[]{:S(2)}) collective-permute-start(f32[7,3,128,512]{3,2,1,0:T(8,128)} %copy.116), channel_id=1, source_target_pairs={{16,0},{17,1},{18,2},{19,3},{20,4},{21,5},{22,6},{23,7},{24,8},{25... | collective-permute-start | bytes 16515080 | tf_op jit(solution)/shard_map/ppermute | solution.py:23
  471.9 121.2 %collective-permute-start = (f32[7,3,128,512]{3,2,1,0:T(8,128)}, f32[7,3,128,512]{3,2,1,0:T(8,128)}, u32[]{:S(2)}, u32[]{:S(2)}) collective-permute-start(f32[7,3,128,512]{3,2,1,0:T(8,128)} %copy.114), channel_id=1, source_target_pairs={{0,16},{1,17},{2,18},{3,19},{4,20},{5,21},{6,22},{7,23},{8,24},{9,... | collective-permute-start | bytes 16515080 | tf_op jit(solution)/shard_map/ppermute | solution.py:22
  583.5 16.9 %slice-start.2 = ((s8[12582912]{0:T(1024)(128)(4,1)}), s8[4194304]{0:T(1024)(128)(4,1)S(1)}, s32[]{:S(2)}) async-start(s8[12582912]{0:T(1024)(128)(4,1)} %bitcast.85), calls=%async_computation.4 | async-start | bytes 8388608
  583.5 16.9 %slice-start.3 = ((s8[12582912]{0:T(1024)(128)(4,1)}), s8[4194304]{0:T(1024)(128)(4,1)S(1)}, s32[]{:S(2)}) async-start(s8[12582912]{0:T(1024)(128)(4,1)} %bitcast.85), calls=%async_computation.5 | async-start | bytes 8388608
  587.1 13.2 %copy-start.6 = (f32[7,3,128,512]{3,2,0,1:T(8,128)}, f32[7,3,128,512]{3,2,0,1:T(8,128)S(1)}, u32[]{:S(2)}) copy-start(f32[7,3,128,512]{3,2,0,1:T(8,128)S(1)} %copy_select_fusion) | copy-start | bytes 16515076
  605.0 27.8 %collective-permute-start.3 = (f32[7,22,3,512]{3,1,2,0:T(8,128)S(1)}, f32[7,22,3,512]{3,1,2,0:T(8,128)S(1)}, u32[]{:S(2)}, u32[]{:S(2)}) collective-permute-start(f32[7,22,3,512]{3,1,2,0:T(8,128)S(1)} %copy.119), channel_id=1, source_target_pairs={{1,0},{2,1},{3,2},{4,3},{5,4},{6,5},{7,6},{8,7},{9,8},{10,9},{11,1... | collective-permute-start | bytes 2838536 | tf_op jit(solution)/shard_map/ppermute | solution.py:23
  607.5 27.1 %collective-permute-start.2 = (f32[7,22,3,512]{3,1,2,0:T(8,128)S(1)}, f32[7,22,3,512]{3,1,2,0:T(8,128)S(1)}, u32[]{:S(2)}, u32[]{:S(2)}) collective-permute-start(f32[7,22,3,512]{3,1,2,0:T(8,128)S(1)} %copy.118), channel_id=1, source_target_pairs={{0,1},{1,2},{2,3},{3,4},{4,5},{5,6},{6,7},{7,8},{8,9},{9,10},{10,1... | collective-permute-start | bytes 2838536 | tf_op jit(solution)/shard_map/ppermute | solution.py:22
  727.2 20.3 %copy-start.1 = (f32[22,134,512]{2,1,0:T(8,128)}, f32[22,134,512]{2,1,0:T(8,128)S(1)}, u32[]{:S(2)}) copy-start(f32[22,134,512]{2,1,0:T(8,128)S(1)} %get-tuple-element.20) | copy-start | bytes 18112516
  836.3 11.2 %slice-start = ((s8[6127616]{0:T(1024)(128)(4,1)}), s8[4194304]{0:T(1024)(128)(4,1)S(1)}, s32[]{:S(2)}) async-start(s8[6127616]{0:T(1024)(128)(4,1)} %bitcast.83), calls=%async_computation.2 | async-start | bytes 8388608
  836.3 11.2 %slice-start.5 = ((s8[6127616]{0:T(1024)(128)(4,1)}), s8[4194304]{0:T(1024)(128)(4,1)S(1)}, s32[]{:S(2)}) async-start(s8[6127616]{0:T(1024)(128)(4,1)} %bitcast.87), calls=%async_computation.7 | async-start | bytes 8388608
  836.9 10.6 %slice-start.1 = ((s8[6127616]{0:T(1024)(128)(4,1)}), s8[1933312]{0:T(1024)(128)(4,1)S(1)}, s32[]{:S(2)}) async-start(s8[6127616]{0:T(1024)(128)(4,1)} %bitcast.83), calls=%async_computation.3 | async-start | bytes 3866624
  836.9 10.6 %slice-start.6 = ((s8[6127616]{0:T(1024)(128)(4,1)}), s8[1933312]{0:T(1024)(128)(4,1)S(1)}, s32[]{:S(2)}) async-start(s8[6127616]{0:T(1024)(128)(4,1)} %bitcast.87), calls=%async_computation.8 | async-start | bytes 3866624
  849.1 21.5 %copy-start.14 = (pred[512]{0:T(512)(128)(4,1)S(1)}, pred[512]{0:T(512)(128)(4,1)}, u32[]{:S(2)}) copy-start(pred[512]{0:T(512)(128)(4,1)} %iota_compare_fusion.3) | copy-start | bytes 1540
  891.6 15.0 %slice-start.7 = ((s8[4456448]{0:T(1024)(128)(4,1)}), s8[4194304]{0:T(1024)(128)(4,1)S(1)}, s32[]{:S(2)}) async-start(s8[4456448]{0:T(1024)(128)(4,1)} %bitcast.89), calls=%async_computation.9 | async-start | bytes 8388608
  891.6 15.0 %slice-start.9 = ((s8[4456448]{0:T(1024)(128)(4,1)}), s8[4194304]{0:T(1024)(128)(4,1)S(1)}, s32[]{:S(2)}) async-start(s8[4456448]{0:T(1024)(128)(4,1)} %bitcast.91), calls=%async_computation.11 | async-start | bytes 8388608
  906.6 11.6 %slice-start.17 = ((s8[5013504]{0:T(1024)(128)(4,1)}), s8[4194304]{0:T(1024)(128)(4,1)S(1)}, s32[]{:S(2)}) async-start(s8[5013504]{0:T(1024)(128)(4,1)} %bitcast.101), calls=%async_computation.19 | async-start | bytes 8388608
  906.7 11.6 %slice-start.18 = ((s8[5013504]{0:T(1024)(128)(4,1)}), s8[819200]{0:T(1024)(128)(4,1)S(1)}, s32[]{:S(2)}) async-start(s8[5013504]{0:T(1024)(128)(4,1)} %bitcast.101), calls=%async_computation.20 | async-start | bytes 1638400
  931.7 48.3 %slice-start.11 = ((s8[6127616]{0:T(1024)(128)(4,1)}), s8[4194304]{0:T(1024)(128)(4,1)S(1)}, s32[]{:S(2)}) async-start(s8[6127616]{0:T(1024)(128)(4,1)} %bitcast.93), calls=%async_computation.13 | async-start | bytes 8388608
  948.2 20.9 %copy-start.10 = (f32[16,128,512]{2,1,0:T(8,128)S(1)}, f32[16,128,512]{2,1,0:T(8,128)}, u32[]{:S(2)}) copy-start(f32[16,128,512]{2,1,0:T(8,128)} %divide_select_fusion) | copy-start | bytes 12582916
  948.2 31.8 %slice-start.12 = ((s8[6127616]{0:T(1024)(128)(4,1)}), s8[1933312]{0:T(1024)(128)(4,1)S(1)}, s32[]{:S(2)}) async-start(s8[6127616]{0:T(1024)(128)(4,1)} %bitcast.93), calls=%async_computation.14 | async-start | bytes 3866624
  969.2 10.8 %copy-start.12 = (f32[17,128,1]{2,1,0:T(8,128)S(1)}, f32[17,128,1]{2,1,0:T(8,128)}, u32[]{:S(2)}) copy-start(f32[17,128,1]{2,1,0:T(8,128)} %get-tuple-element.58) | copy-start | bytes 26116
  969.2 10.8 %copy-start.13 = (f32[16,129,1]{2,1,0:T(8,128)S(1)}, f32[16,129,1]{2,1,0:T(8,128)}, u32[]{:S(2)}) copy-start(f32[16,129,1]{2,1,0:T(8,128)} %get-tuple-element.61) | copy-start | bytes 24772
  (24 other events, 159.3 us)
where the time goes:
time: 1020 us
  other arithmetic  409 us (40%)
  waiting for transfers between devices  232 us (23%)
  local copies, waits for them, and re-layouts  220 us (22%)
  matrix products  128 us (13%)
  starting transfers between devices  25 us (2%)
    ppermute x2, waiting for transfers between devices, extended(): after = lax.ppermute(leading, axis, down)  128 us
    dot_general x1, matrix products, per_device(): lax.dot_general(spectrum.reshape(-1, NP), fourier_basis, (((1,), (1,)), (...  94.4 us
    all_to_all x1, waiting for transfers between devices, per_device(): lax.all_to_all(smoothed, 'phi', split_axis=3, concat_axis=2, tiled=True)  78.6 us
    dot_general x1, other arithmetic, per_device(): jnp.dot(lines.reshape(-1, NP), fourier_basis, precision=lax.Precision.HIG...  67.5 us
    concatenate x1, other arithmetic, extended(): value = jnp.concatenate([before, value, after], axis=dim)  57.4 us
    unnamed x86, local copies, waits for them, and re-layouts  55.7 us
    sub x2, other arithmetic, edge_values(): to_right = right_face - centre  39.5 us
    div x2, other arithmetic, hll_flux(): (upwind + slowest * fastest * (dens_right - dens_left)) / (fastest - slow...  37.5 us
  transfers between devices with their start and end apart: 6, of which 5 were waited for; matrix products, arithmetic and copies ran while one was open for 9% of the time, Pallas kernels for 0%

commit v1 on v0

--- a/solution.py
+++ b/solution.py
@@ -221,7 +221,10 @@
         precision=lax.Precision.HIGHEST,
         preferred_element_type=jnp.float32,
     ).reshape(lines.shape)
-    returned = lax.all_to_all(smoothed, "phi", split_axis=3, concat_axis=2, tiled=True)
+    returned = jnp.concatenate(
+        lax.all_to_all(jnp.stack(jnp.split(smoothed, lax.axis_size("phi"), axis=3)), "phi", 0, 0),
+        axis=2,
+    )
     returned = jnp.swapaxes(returned, 2, 3)
     primitive = jnp.concatenate(
         [

time: 1020 us -> 924 us (0.906)
  local copies, waits for them, and re-layouts: 220 us -> 137 us
  other arithmetic: 409 us -> 396 us
    unnamed x86 -> x99, local copies, waits for them, and re-layouts: 55.7 us -> 19 us
    dot_general x1 -> x0, local copies, waits for them, and re-layouts: 26.4 us -> none  [per_device(): lax.dot_general(spectrum.reshape(-1, NP), fourier_basis, (((1,), (1,)), (...]
    all_to_all x2 -> x0, local copies, waits for them, and re-layouts: 21.6 us -> none  [per_device(): lax.all_to_all(smoothed, 'phi', split_axis=3, concat_axis=2, tiled=True)]
    all_to_all x1 -> x0, other arithmetic: 13.7 us -> none  [per_device(): lax.all_to_all(smoothed, 'phi', split_axis=3, concat_axis=2, tiled=True)]
  transfers between devices with their start and end apart: 6 -> 6, of which waited for: 5 -> 5; matrix products, arithmetic and copies ran while one was open for 9% -> 10% of each run, Pallas kernels for 0% -> 0%
where the time goes in v1:
time: 924 us; the launch traced here: 919 us
  other arithmetic  396 us (43%)
  waiting for transfers between devices  232 us (25%)
  local copies, waits for them, and re-layouts  137 us (15%)
  matrix products  128 us (14%)
  starting transfers between devices  25.1 us (3%)
    ppermute x2, waiting for transfers between devices, extended(): after = lax.ppermute(leading, axis, down)  128 us
    dot_general x1, matrix products, per_device(): lax.dot_general(spectrum.reshape(-1, NP), fourier_basis, (((1,), (1,)), (...  93.7 us
    all_to_all x1, waiting for transfers between devices, per_device(): lax.all_to_all(jnp.stack(jnp.split(smoothed, lax.axis_size('phi'), axis=3...  78.6 us
    dot_general x1, other arithmetic, per_device(): jnp.dot(lines.reshape(-1, NP), fourier_basis, precision=lax.Precision.HIG...  67.5 us
    concatenate x1, other arithmetic, extended(): value = jnp.concatenate([before, value, after], axis=dim)  57.5 us
    sub x2, other arithmetic, edge_values(): to_right = right_face - centre  39.5 us
    div x2, other arithmetic, hll_flux(): (upwind + slowest * fastest * (dens_right - dens_left)) / (fastest - slow...  37.3 us
    another operation x2, other arithmetic, advance(): return (density_next, jnp.stack([radial_next, polar_next, azimuth_next]))  36.3 us
  transfers between devices with their start and end apart: 6, of which 5 were waited for; matrix products, arithmetic and copies ran while one was open for 10% of the time, Pallas kernels for 0%

profile of v1, /device:TPU:13, one launch (start us, length us, event | category | flops | bytes accessed | tf_op | source)
XLA Modules:
  0.0 918.6 jit_solution(13087565515550808105)
XLA Ops:
  20.5 67.5 %fusion.169 = f32[2048,2048,1,1]{1,0,3,2:T(8,128)} fusion(s32[2048]{0:T(1024)S(1)} %iota_add_fusion, pred[2048]{0:T(1024)(128)(4,1)S(1)} %iota_compare_fusion.2), kind=kLoop, calls=%fused_computation.10.clone.1 | loop fusion | flops 67108864 | bytes 16787456 | tf_op jit(solution)/shard_map/dot_general | solution.py:210
  88.0 20.2 %all-to-all-done = f32[4,16,128,128]{3,1,0,2:T(8,128)} async-done(((f32[4,16,128,128]{3,1,0,2:T(8,128)}), f32[4,16,128,128]{3,1,0,2:T(8,128)}, u32[]{:S(2)}, u32[]{:S(2)}) %all-to-all-start) | async-done | bytes 4194336 | tf_op jit(solution)/shard_map/all_to_all | solution.py:202
  108.2 33.9 %fusion.5 = f32[4,16,8,2048]{3,2,1,0:T(8,128)S(1)} fusion(f32[4,16,128,128]{3,1,0,2:T(8,128)} %all-to-all-done, f32[2048,2048,1,1]{1,0,3,2:T(8,128)} %fusion.169), kind=kOutput, calls=%fused_computation.9 | convolution fusion | flops 25769803776 | bytes 25165824 | tf_op jit(solution)/shard_map/dot_general | solution.py:210
  142.4 93.7 %fusion.3 = f32[4,16,8,2048]{3,2,1,0:T(8,128)S(1)} fusion(pred[2048]{0:T(1024)(128)(4,1)S(1)} %iota_compare_fusion.2, s32[2048]{0:T(1024)S(1)} %iota_add_fusion, f32[4,16,8,2048]{3,2,1,0:T(8,128)S(1)} %fusion.167), kind=kOutput, calls=%fused_computation.7 | convolution fusion | flops 25836912640 | bytes 8398848 | tf_op jit(solution)/shard_map/dot_general | solution.py:217
  255.0 11.6 %pad_maximum_fusion.1 = f32[4,16,128,384]{3,2,0,1:T(8,128)} fusion(f32[1,16,128,512]{3,2,0,1:T(8,128)} %bitcast.174, f32[3,16,128,512]{3,2,1,0:T(8,128)} %param.4), kind=kLoop, calls=%fused_computation.13 | loop fusion | flops 3145728 | bytes 29360128 | tf_op jit(solution)/shard_map/concatenate | solution.py:185
  266.6 78.6 %all-to-all-done.1 = f32[16,4,16,8,128]{4,3,2,1,0:T(8,128)} async-done(((f32[16,4,16,8,128]{4,3,2,1,0:T(8,128)}), f32[16,4,16,8,128]{4,3,2,1,0:T(8,128)}, u32[]{:S(2)}, u32[]{:S(2)}) %all-to-all-start.1) | async-done | bytes 4194336 | tf_op jit(solution)/shard_map/all_to_all | solution.py:225
  379.2 106.2 %collective-permute-done.1 = f32[7,3,128,512]{3,2,1,0:T(8,128)} collective-permute-done((f32[7,3,128,512]{3,2,1,0:T(8,128)}, f32[7,3,128,512]{3,2,1,0:T(8,128)}, u32[]{:S(2)}, u32[]{:S(2)}) %collective-permute-start.1) | collective-permute-done | bytes 5505056 | tf_op jit(solution)/shard_map/ppermute | solution.py:23
  494.8 7.3 copy_select_fusion.1
  513.4 21.5 %collective-permute-done.3 = f32[7,22,3,512]{3,1,2,0:T(8,128)S(1)} collective-permute-done((f32[7,22,3,512]{3,1,2,0:T(8,128)S(1)}, f32[7,22,3,512]{3,1,2,0:T(8,128)S(1)}, u32[]{:S(2)}, u32[]{:S(2)}) %collective-permute-start.3) | collective-permute-done | bytes 946208 | tf_op jit(solution)/shard_map/ppermute | solution.py:23
  538.2 57.5 %pad_maximum_fusion = f32[7,22,134,512]{3,2,0,1:T(8,128)} fusion(f32[7,22,3,512]{3,2,0,1:T(4,128)} %copy.99, f32[7,3,128,512]{3,2,0,1:T(8,128)} %copy-done.6, f32[4,16,128,64]{3,2,0,1:T(8,128)S(1)} %copy-done.2, f32[4,16,128,384]{3,2,0,1:T(8,128)S(1)} %bitcast.148, f32[4,16,128,64]{3,2,0,1:T(8,128)} %copy.89, f32[7,3,128,512]{3,2,0,1:T(8,128)} %copy_select_fusion.1, ...), kind=kLoop, calls=%fused_computation | loop fusion | flops 73959424 | bytes 84525056 | tf_op jit(solution)/shard_map/concatenate | solution.py:24
  595.7 8.2 slice_bitcast_fusion.8
  603.9 25.5 %slice_bitcast_fusion.3 = (f32[22,134,512]{2,1,0:T(8,128)}, f32[22,134,512]{2,1,0:T(8,128)}, f32[22,134,512]{2,1,0:T(8,128)S(1)}, f32[22,134,512]{2,1,0:T(8,128)...) fusion(f32[7,22,134,512]{3,2,0,1:T(8,128)} %pad_maximum_fusion), kind=kLoop, calls=%fused_computation.18 | loop fusion | bytes 84525056 | tf_op jit(solution)/shard_map/squeeze | solution.py:149
  659.6 27.9 %fusion.15 = (f32[18,128,512]{2,1,0:T(8,128)}, f32[18,128,512]{2,1,0:T(8,128)}, f32[18,128,512]{2,1,0:T(8,128)}, f32[18,128,512]{2,1,0:T(8,128)}, f32[18,128,512]{2,1,0:T(8,128)}, /*index=5*/f32[18,128,512]{2,1,0:T(8,128)}) fusion(f32[22,134,512]{2,1,0:T(8,128)} %copy-done, f32[22,134,512]{2,1,0:T(8,128)} %get-tuple-element.19), kind=kLoop, calls=%fused_computation.46 | loop fusion | flops 47185920 | bytes 75497472 | tf_op jit(solution)/shard_map/sub | solution.py:50
  687.5 15.3 %subtract_negate_fusion.1 = f32[18,130,512]{2,1,0:T(8,128)} fusion(f32[22,134,512]{2,1,0:T(8,128)} %get-tuple-element.22, f32[22,134,512]{2,1,0:T(8,128)} %get-tuple-element.19, f32[22,134,512]{2,1,0:T(8,128)} %get-tuple-element.16, f32[22,134,512]{2,1,0:T(8,128)} %get-tuple-element.21), kind=kLoop, calls=%fused_computation.35 | loop fusion | flops 9584640 | bytes 33546240 | tf_op jit(solution)/shard_map/neg | solution.py:137
  702.8 23.6 %subtract_negate_fusion.2 = (f32[18,130,512]{2,1,0:T(8,128)}, f32[18,130,512]{2,1,0:T(8,128)}) fusion(f32[22,134,512]{2,1,0:T(8,128)} %copy-done.1, f32[22,134,512]{2,1,0:T(8,128)} %get-tuple-element.19, f32[22,134,512]{2,1,0:T(8,128)} %get-tuple-element.16, f32[18,130,1]{2,1,0:T(8,128)S(1)} %slice.613, f32[18,130,511]{2,1,0:T(8,128)} %slice.612, ...), kind=kLoop, calls=%fused_computation.36 | loop fusion | flops 17971200 | bytes 52715520 | tf_op jit(solution)/shard_map/neg | solution.py:138
  751.1 16.7 %minimum_add_fusion = (f32[16,128,512]{2,1,0:T(8,128)}, f32[16,128,512]{2,1,0:T(8,128)}) fusion(f32[16,128,2]{2,1,0:T(8,128)S(1)} %reshape.121, f32[16,128,510]{2,1,0:T(8,128)S(1)} %copy-done.9, f32[16,128,510]{2,1,0:T(8,128)S(1)} %copy-done.7, f32[16,128,2]{2,1,0:T(8,128)S(1)} %reshape.120, f32[22,134,512]{2,1,0:T(8,128)S(1)} %bitcast.146, ...), kind=kLoop, calls=%fused_computation.207 | loop fusion | flops 62914560 | bytes 50331648 | tf_op jit(solution)/shard_map/add | solution.py:53
  772.6 21.2 %divide_select_fusion = f32[16,128,512]{2,1,0:T(8,128)} fusion(f32[16,128,511]{2,1,0:T(8,128)} %bitcast.171, f32[16,128,1]{2,1,0:T(8,128)} %slice.578, f32[16,128,2]{2,1,0:T(8,128)S(1)} %reshape.121, f32[16,128,510]{2,1,0:T(8,128)} %get-tuple-element.44, f32[16,128,510]{2,1,0:T(8,128)S(1)} %copy-done.8, f32[16,128,2]{2,1,0:T(8,128)S(1)} %reshape.120, ...), kind=kLoop, calls=%fused_computation.206 | loop fusion | flops 83886080 | bytes 54526464 | tf_op jit(solution)/shard_map/jit(_where)/select_n | solution.py:95
  799.3 9.5 %fusion.10 = f32[17,129,512]{2,1,0:T(8,128)} fusion(f32[18,130,512]{2,1,0:T(8,128)} %subtract_negate_fusion.1), kind=kLoop, calls=%fused_computation.38 | loop fusion | flops 4491264 | bytes 22456320 | tf_op jit(solution)/shard_map/mul | solution.py:145
  808.9 11.6 %fusion.39 = (f32[16,130,512]{2,1,0:T(8,128)}, f32[16,130,512]{2,1,0:T(8,128)}, f32[16,130,512]{2,1,0:T(8,128)}, f32[16,130,512]{2,1,0:T(8,128)}, f32[16,130,512]{2,1,0:T(8,128)}, /*index=5*/f32[16,130,512]{2,1,0:T(8,128)}) fusion(f32[16,134,512]{2,1,0:T(8,128)S(1)} %bitcast.154, f32[16,134,512]{2,1,0:T(8,128)S(1)} %bitcast.152), kind=kLoop, calls=%fused_computation.82 | loop fusion | flops 42598400 | bytes 68157440 | tf_op jit(solution)/shard_map/sub | solution.py:50
  834.0 16.5 %subtract_divide_fusion = f32[16,129,512]{2,1,0:T(8,128)} fusion(f32[16,130,512]{2,1,0:T(8,128)S(1)} %bitcast.168, f32[16,130,512]{2,1,0:T(8,128)S(1)} %bitcast.170, f32[16,130,512]{2,1,0:T(8,128)S(1)} %bitcast.166, f32[16,130,512]{2,1,0:T(8,128)} %get-tuple-element.71, f32[16,130,512]{2,1,0:T(8,128)} %get-tuple-element.70, ...), kind=kLoop, calls=%fused_computation.131 | loop fusion | flops 43327488 | bytes 54951936 | tf_op jit(solution)/shard_map/div | solution.py:60
  850.5 20.8 %subtract_divide_fusion.1 = f32[17,128,512]{2,1,0:T(8,128)} fusion(f32[18,128,512]{2,1,0:T(8,128)} %get-tuple-element.49, f32[18,128,512]{2,1,0:T(8,128)} %get-tuple-element.50, f32[18,128,512]{2,1,0:T(8,128)} %get-tuple-element.48, f32[18,128,512]{2,1,0:T(8,128)} %get-tuple-element.74, f32[18,128,512]{2,1,0:T(8,128)} %get-tuple-element.73, ...), kind=kLoop, calls=%fused_computation.132 | loop fusion | flops 45678592 | bytes 57933824 | tf_op jit(solution)/shard_map/div | solution.py:60
  871.3 10.8 %fusion.83 = f32[16,128,512]{2,1,0:T(8,128)} fusion(f32[16,129,512]{2,1,0:T(8,128)} %subtract_divide_fusion, f32[17,128,512]{2,1,0:T(8,128)} %subtract_divide_fusion.1, f32[16,128,512]{2,1,0:T(8,128)S(1)} %copy-done.10, f32[16,128,511]{2,1,0:T(8,128)} %slice.580, f32[22,134,512]{2,1,0:T(8,128)S(1)} %bitcast.146), kind=kLoop, calls=%fused_computation.162 | loop fusion | flops 9437184 | bytes 33546240 | tf_op jit(solution)/shard_map/sub | solution.py:121
  882.2 24.2 %fusion.77 = (f32[1,16,128,512]{3,2,1,0:T(8,128)}, f32[1,16,128,512]{3,2,1,0:T(8,128)}, f32[1,16,128,512]{3,2,1,0:T(8,128)}) fusion(f32[17,129,512]{2,1,0:T(8,128)} %fusion.10, f32[17,128,512]{2,1,0:T(8,128)} %copy-done.4, f32[17,128,1]{2,1,0:T(8,128)S(1)} %copy-done.12, f32[17,128,511]{2,1,0:T(8,128)} %get-tuple-element.54, ...), kind=kLoop, calls=%fused_computation.153 | loop fusion | flops 25165824 | bytes 71598080 | tf_op jit(solution)/shard_map/stack | solution.py:163
  906.3 12.1 %pad_maximum_fusion.2 = f32[3,16,128,512]{3,2,1,0:T(8,128)} fusion(f32[1,16,128,512]{3,2,1,0:T(8,128)} %get-tuple-element.52, f32[1,16,128,512]{3,2,1,0:T(8,128)} %get-tuple-element.53, f32[1,16,128,512]{3,2,1,0:T(8,128)} %get-tuple-element.51), kind=kLoop, calls=%fused_computation.14 | loop fusion | flops 6291456 | bytes 25165824 | tf_op jit(solution)/shard_map/stack | solution.py:163
  (168 shorter events, 175.4 us)
Async XLA Ops:
  11.4 96.8 %all-to-all-start = ((f32[4,16,128,128]{3,1,0,2:T(8,128)}), f32[4,16,128,128]{3,1,0,2:T(8,128)}, u32[]{:S(2)}, u32[]{:S(2)}) async-start(f32[4,16,128,128]{3,1,0,2:T(8,128)} %copy.86), calls=%async_computation | async-start | bytes 8388608 | tf_op jit(solution)/shard_map/all_to_all | solution.py:202
  247.9 97.2 %all-to-all-start.1 = ((f32[16,4,16,8,128]{4,3,2,1,0:T(8,128)}), f32[16,4,16,8,128]{4,3,2,1,0:T(8,128)}, u32[]{:S(2)}, u32[]{:S(2)}) async-start(f32[16,4,16,8,128]{4,3,2,1,0:T(8,128)} %fusion.113), calls=%async_computation.1 | async-start | bytes 8388608 | tf_op jit(solution)/shard_map/all_to_all | solution.py:225
  365.9 119.5 %collective-permute-start.1 = (f32[7,3,128,512]{3,2,1,0:T(8,128)}, f32[7,3,128,512]{3,2,1,0:T(8,128)}, u32[]{:S(2)}, u32[]{:S(2)}) collective-permute-start(f32[7,3,128,512]{3,2,1,0:T(8,128)} %copy.94), channel_id=1, source_target_pairs={{16,0},{17,1},{18,2},{19,3},{20,4},{21,5},{22,6},{23,7},{24,8},{25... | collective-permute-start | bytes 16515080 | tf_op jit(solution)/shard_map/ppermute | solution.py:23
  373.6 121.2 %collective-permute-start = (f32[7,3,128,512]{3,2,1,0:T(8,128)}, f32[7,3,128,512]{3,2,1,0:T(8,128)}, u32[]{:S(2)}, u32[]{:S(2)}) collective-permute-start(f32[7,3,128,512]{3,2,1,0:T(8,128)} %copy.92), channel_id=1, source_target_pairs={{0,16},{1,17},{2,18},{3,19},{4,20},{5,21},{6,22},{7,23},{8,24},{9,... | collective-permute-start | bytes 16515080 | tf_op jit(solution)/shard_map/ppermute | solution.py:22
  485.4 16.7 %slice-start.2 = ((s8[12582912]{0:T(1024)(128)(4,1)}), s8[4194304]{0:T(1024)(128)(4,1)S(1)}, s32[]{:S(2)}) async-start(s8[12582912]{0:T(1024)(128)(4,1)} %bitcast.147), calls=%async_computation.4 | async-start | bytes 8388608
  485.4 16.7 %slice-start.3 = ((s8[12582912]{0:T(1024)(128)(4,1)}), s8[4194304]{0:T(1024)(128)(4,1)S(1)}, s32[]{:S(2)}) async-start(s8[12582912]{0:T(1024)(128)(4,1)} %bitcast.147), calls=%async_computation.5 | async-start | bytes 8388608
  489.0 13.1 %copy-start.6 = (f32[7,3,128,512]{3,2,0,1:T(8,128)}, f32[7,3,128,512]{3,2,0,1:T(8,128)S(1)}, u32[]{:S(2)}) copy-start(f32[7,3,128,512]{3,2,0,1:T(8,128)S(1)} %copy_select_fusion) | copy-start | bytes 16515076
  506.8 28.1 %collective-permute-start.3 = (f32[7,22,3,512]{3,1,2,0:T(8,128)S(1)}, f32[7,22,3,512]{3,1,2,0:T(8,128)S(1)}, u32[]{:S(2)}, u32[]{:S(2)}) collective-permute-start(f32[7,22,3,512]{3,1,2,0:T(8,128)S(1)} %copy.97), channel_id=1, source_target_pairs={{1,0},{2,1},{3,2},{4,3},{5,4},{6,5},{7,6},{8,7},{9,8},{10,9},{11,1... | collective-permute-start | bytes 2838536 | tf_op jit(solution)/shard_map/ppermute | solution.py:23
  509.2 27.3 %collective-permute-start.2 = (f32[7,22,3,512]{3,1,2,0:T(8,128)S(1)}, f32[7,22,3,512]{3,1,2,0:T(8,128)S(1)}, u32[]{:S(2)}, u32[]{:S(2)}) collective-permute-start(f32[7,22,3,512]{3,1,2,0:T(8,128)S(1)} %copy.96), channel_id=1, source_target_pairs={{0,1},{1,2},{2,3},{3,4},{4,5},{5,6},{6,7},{7,8},{8,9},{9,10},{10,1... | collective-permute-start | bytes 2838536 | tf_op jit(solution)/shard_map/ppermute | solution.py:22
  629.4 20.3 %copy-start.1 = (f32[22,134,512]{2,1,0:T(8,128)}, f32[22,134,512]{2,1,0:T(8,128)S(1)}, u32[]{:S(2)}) copy-start(f32[22,134,512]{2,1,0:T(8,128)S(1)} %get-tuple-element.18) | copy-start | bytes 18112516
  644.4 10.6 %slice-start.19 = ((s8[6127616]{0:T(1024)(128)(4,1)}), s8[4194304]{0:T(1024)(128)(4,1)S(1)}, s32[]{:S(2)}) async-start(s8[6127616]{0:T(1024)(128)(4,1)} %bitcast.163), calls=%async_computation.21 | async-start | bytes 8388608
  738.3 11.2 %slice-start = ((s8[6127616]{0:T(1024)(128)(4,1)}), s8[4194304]{0:T(1024)(128)(4,1)S(1)}, s32[]{:S(2)}) async-start(s8[6127616]{0:T(1024)(128)(4,1)} %bitcast.145), calls=%async_computation.2 | async-start | bytes 8388608
  738.3 11.2 %slice-start.5 = ((s8[6127616]{0:T(1024)(128)(4,1)}), s8[4194304]{0:T(1024)(128)(4,1)S(1)}, s32[]{:S(2)}) async-start(s8[6127616]{0:T(1024)(128)(4,1)} %bitcast.149), calls=%async_computation.7 | async-start | bytes 8388608
  738.9 10.5 %slice-start.1 = ((s8[6127616]{0:T(1024)(128)(4,1)}), s8[1933312]{0:T(1024)(128)(4,1)S(1)}, s32[]{:S(2)}) async-start(s8[6127616]{0:T(1024)(128)(4,1)} %bitcast.145), calls=%async_computation.3 | async-start | bytes 3866624
  751.1 21.5 %copy-start.14 = (pred[512]{0:T(512)(128)(4,1)S(1)}, pred[512]{0:T(512)(128)(4,1)}, u32[]{:S(2)}) copy-start(pred[512]{0:T(512)(128)(4,1)} %iota_compare_fusion.3) | copy-start | bytes 1540
  793.8 15.0 %slice-start.7 = ((s8[4456448]{0:T(1024)(128)(4,1)}), s8[4194304]{0:T(1024)(128)(4,1)S(1)}, s32[]{:S(2)}) async-start(s8[4456448]{0:T(1024)(128)(4,1)} %bitcast.151), calls=%async_computation.9 | async-start | bytes 8388608
  793.8 15.0 %slice-start.9 = ((s8[4456448]{0:T(1024)(128)(4,1)}), s8[4194304]{0:T(1024)(128)(4,1)S(1)}, s32[]{:S(2)}) async-start(s8[4456448]{0:T(1024)(128)(4,1)} %bitcast.153), calls=%async_computation.11 | async-start | bytes 8388608
  808.8 11.7 %slice-start.17 = ((s8[5013504]{0:T(1024)(128)(4,1)}), s8[4194304]{0:T(1024)(128)(4,1)S(1)}, s32[]{:S(2)}) async-start(s8[5013504]{0:T(1024)(128)(4,1)} %bitcast.161), calls=%async_computation.19 | async-start | bytes 8388608
  808.9 11.6 %slice-start.18 = ((s8[5013504]{0:T(1024)(128)(4,1)}), s8[819200]{0:T(1024)(128)(4,1)S(1)}, s32[]{:S(2)}) async-start(s8[5013504]{0:T(1024)(128)(4,1)} %bitcast.161), calls=%async_computation.20 | async-start | bytes 1638400
  834.0 48.1 %slice-start.11 = ((s8[6127616]{0:T(1024)(128)(4,1)}), s8[4194304]{0:T(1024)(128)(4,1)S(1)}, s32[]{:S(2)}) async-start(s8[6127616]{0:T(1024)(128)(4,1)} %bitcast.155), calls=%async_computation.13 | async-start | bytes 8388608
  850.5 20.8 %copy-start.10 = (f32[16,128,512]{2,1,0:T(8,128)S(1)}, f32[16,128,512]{2,1,0:T(8,128)}, u32[]{:S(2)}) copy-start(f32[16,128,512]{2,1,0:T(8,128)} %divide_select_fusion) | copy-start | bytes 12582916
  850.5 31.7 %slice-start.12 = ((s8[6127616]{0:T(1024)(128)(4,1)}), s8[1933312]{0:T(1024)(128)(4,1)S(1)}, s32[]{:S(2)}) async-start(s8[6127616]{0:T(1024)(128)(4,1)} %bitcast.155), calls=%async_computation.14 | async-start | bytes 3866624
  871.3 10.9 %copy-start.12 = (f32[17,128,1]{2,1,0:T(8,128)S(1)}, f32[17,128,1]{2,1,0:T(8,128)}, u32[]{:S(2)}) copy-start(f32[17,128,1]{2,1,0:T(8,128)} %get-tuple-element.56) | copy-start | bytes 26116
  871.3 10.9 %copy-start.13 = (f32[16,129,1]{2,1,0:T(8,128)S(1)}, f32[16,129,1]{2,1,0:T(8,128)}, u32[]{:S(2)}) copy-start(f32[16,129,1]{2,1,0:T(8,128)} %get-tuple-element.59) | copy-start | bytes 24772
  (24 other events, 159.4 us)
